TPU v7x, 128 devices: a whole 4x4x4 slice. The times are simulated.
128 devices in a mesh: section: 2 (over core), tp: 4 (over x), pool: 16 (over z, y).
Axes of the slice: x: 4, y: 4, z: 4, core: 2. Of those that a mesh axis runs over, the one named last changes fastest.
Arguments:
- hidden: bfloat16 [2, 16, 128, 8192], P('section', 'pool', None, 'tp'), may hold values from -6 to 6
- queries: bfloat16 [2, 16, 16, 8, 64, 128], P('section', 'pool', None, None, 'tp'), may hold values from -450 to 450, as said below
- window_key_value: bfloat16 [2, 16, 16, 2, 8, 8, 128], P('section', 'pool', None, None, 'tp'), may hold values from -12 to 12
- cached_key_value: bfloat16 [2, 16, 128, 2, 8, 64, 128], P('section', 'pool', None, None, 'tp'), may hold values from -12 to 12
- cached_length: int32 [2, 16, 16], P('section', 'pool'), may hold values from 1 to 1024, 6144 in all within a row
- request_page_table: int32 [2, 16, 16, 16], P('section', 'pool'), may hold values from 0 to 127
- request_adapter: int32 [2, 16, 16], replicated, may hold values from 0 to 127, as said below
- layer_page_slot: int32 [256], replicated, may hold values from 0 to 255, as said below
- wo: bfloat16 [2, 8192, 8192], P('section', 'tp'), may hold values from -0.09375 to 0.09375
- adapter_down: bfloat16 [256, 64, 8192], P(('section', 'pool'), None, 'tp'), may hold values from -0.0625 to 0.0625
- adapter_up: bfloat16 [256, 64, 8192], P(('section', 'pool'), None, 'tp'), may hold values from -0.75 to 0.75
Outputs:
- next_hidden: bfloat16 [2, 16, 128, 8192], P('section', 'pool', None, 'tp')
Inputs may be any that keep to these rules, and one draw needn't show every extreme that they name: `queries`: queries of order one; some entries far larger in the hidden draw. `request_page_table`: several requests may name the same cache page; entries past a request's length are read but excluded. `cached_length`: each request of a device has 1 to 1024 cached positions. `layer_page_slot`: the adapters of layer s occupy slots s * 128 to (s + 1) * 128 - 1, each slot once; slot q lies on the index q // 8 of section and pool taken together, section first, so layer s's pages sit on section s. `request_adapter`: up to all 16 requests of a pool group may use adapters held on one pool index, and one pool index may serve every request of its section.
All inputs are finite; a program needn't handle non-finite values.
Results may differ from a plain program's by a relative error of at most 0.009.
Values may be sent and summed in bfloat16 or wider, within the bound.
A program may use at most 192 MiB of HBM per device.

v0:
```python
import jax
import jax.numpy as jnp
from jax import lax
from jax.sharding import PartitionSpec as P


def from_behind(value, axis, steps):
    count = lax.axis_size(axis)
    pairs = [(source, (source + steps) % count) for source in range(count)]
    return lax.ppermute(value, axis, pairs)


def attend(queries, cache_pages, window_kv, lengths, page_rows):
    requests, window, head_count, head_size = queries.shape
    kv_heads = window_kv.shape[2]
    page_tok = cache_pages.shape[3]
    max_pages = page_rows.shape[1]
    cached = max_pages * page_tok
    picked = jnp.take(cache_pages, page_rows, axis=0)
    picked = jnp.transpose(picked, (0, 2, 3, 1, 4, 5)).reshape(
        requests, 2, kv_heads, cached, head_size
    )
    keys_all = jnp.concatenate([picked, window_kv], axis=3)
    grouped = queries.reshape(requests, window, kv_heads, head_count // kv_heads, head_size)
    scores = jnp.einsum(
        "rwkgd,rktd->rkgwt", grouped, keys_all[:, 0], preferred_element_type=jnp.float32
    ) * head_size ** (-0.5)
    position = jnp.arange(cached + window, dtype=jnp.int32)
    query_pos = jnp.arange(window, dtype=jnp.int32)
    in_cache = position[None, :] < lengths[:, None]
    in_window = (position[None, :] >= cached) & (position[None, :] - cached <= query_pos[:, None])
    allowed = in_cache[:, None, :] | in_window[None, :, :]
    scores = jnp.where(allowed[:, None, None, :, :], scores, -jnp.inf)
    largest = jnp.max(scores, axis=-1, keepdims=True)
    weights = jnp.exp(scores - largest)
    probs = (weights / jnp.sum(weights, axis=-1, keepdims=True)).astype(jnp.bfloat16)
    context = jnp.einsum(
        "rkgwt,rktd->rwkgd", probs, keys_all[:, 1], preferred_element_type=jnp.float32
    )
    return context.reshape(requests, window, head_count * head_size).astype(jnp.bfloat16)


def per_device(
    hidden,
    queries,
    window_key_value,
    cached_key_value,
    cached_length,
    request_page_table,
    request_adapter,
    layer_page_slot,
    wo,
    adapter_down,
    adapter_up,
):
    section_count = lax.axis_size("section")
    section_index = lax.axis_index("section")
    pool_index = lax.axis_index("pool")
    context = attend(
        queries[0, 0],
        cached_key_value[0, 0],
        window_key_value[0, 0],
        cached_length[0, 0],
        request_page_table[0, 0],
    )
    requests, window, width_of_head = context.shape
    flat_rows = context.reshape(requests * window, width_of_head)
    partial_out = jnp.dot(flat_rows, wo[0], preferred_element_type=jnp.float32)
    plain_output = lax.psum_scatter(partial_out, "tp", scatter_dimension=1, tiled=True)
    pages_per_member = adapter_down.shape[0]
    rank_width = adapter_down.shape[1]
    output_width = adapter_up.shape[2]
    adapters = layer_page_slot.shape[0] // section_count
    layer_start = section_index * adapters
    everyone = lax.all_gather(context, "pool", axis=0, tiled=True)
    total_requests = everyone.shape[0]
    all_slots = layer_page_slot[layer_start + request_adapter[section_index]].reshape(
        total_requests
    )
    local_slot = all_slots - layer_start - pool_index * pages_per_member
    owned_mask = (
        local_slot[:, None] == jnp.arange(pages_per_member, dtype=jnp.int32)[None, :]
    ).astype(jnp.float32)
    stacked_down = adapter_down.reshape(pages_per_member * rank_width, width_of_head)
    wide_rank = lax.dot_general(
        everyone, stacked_down, (((2,), (1,)), ((), ())), preferred_element_type=jnp.float32
    )
    wide_rank = wide_rank.reshape(total_requests, window, pages_per_member, rank_width)
    rank_hidden = jnp.sum(wide_rank * owned_mask[:, None, :, None], axis=2)
    rank_hidden = lax.psum(rank_hidden, "tp")
    broadcast_rows = (
        rank_hidden.astype(jnp.bfloat16)[:, :, None, :]
        * owned_mask.astype(jnp.bfloat16)[:, None, :, None]
    )
    broadcast_rows = broadcast_rows.reshape(total_requests * window, pages_per_member * rank_width)
    product = jnp.dot(
        broadcast_rows,
        adapter_up.reshape(pages_per_member * rank_width, output_width),
        preferred_element_type=jnp.float32,
    )
    returned = lax.all_to_all(
        product.astype(jnp.bfloat16), "pool", split_axis=0, concat_axis=0, tiled=True
    )
    adapter_delta = jnp.sum(
        returned.reshape(-1, requests * window, output_width).astype(jnp.float32), axis=0
    )
    blended_output = (hidden[0, 0].astype(jnp.float32) + plain_output + adapter_delta).astype(
        jnp.bfloat16
    )
    handed = from_behind(blended_output, "section", 1)
    return handed[None, None]


def solution(mesh):
    return jax.shard_map(
        per_device,
        mesh=mesh,
        in_specs=(
            P("section", "pool", None, "tp"),
            P("section", "pool", None, None, "tp", None),
            P("section", "pool", None, None, "tp", None, None),
            P("section", "pool", None, None, "tp", None, None),
            P("section", "pool", None),
            P("section", "pool", None, None),
            P(),
            P(),
            P("section", "tp", None),
            P(("section", "pool"), None, "tp"),
            P(("section", "pool"), None, "tp"),
        ),
        out_specs=P("section", "pool", None, "tp"),
        check_vma=False,
    )
```

profile of v0, /device:TPU:35, one launch (start us, length us, event | category | flops | bytes accessed | tf_op | source)
XLA Modules:
  0.0 320.7 jit_solution(6340486119828184799)
XLA Ops:
  7.4 0.8 compare_select_fusion.1
  9.0 0.9 copy.45
  9.9 0.7 iota_compare_fusion
  10.7 13.1 %gather_fusion = bf16[256,2,2,64,128]{4,3,2,1,0:T(8,128)(2,1)} fusion(bf16[128,2,2,64,128]{4,3,2,1,0:T(8,128)(2,1)} %bitcast.82, s32[1024]{0:T(1024)S(1)} %pad_clamp_fusion.1), kind=kCustom, calls=%fused_computation | custom fusion | bytes 33555456 | tf_op jit(solution)/shard_map/jit(_take)/gather | solution.py:19
  23.8 14.2 %copy_select_fusion = bf16[16,16,2,2,64,128]{5,4,1,3,0,2:T(8,128)(2,1)} fusion(bf16[16,16,2,2,64,128]{5,4,3,2,1,0:T(8,128)(2,1)} %bitcast.81, pred[16,16]{1,0:T(8,128)(4,1)S(1)} %compare_and_fusion), kind=kLoop, calls=%fused_computation.7 | loop fusion | flops 8388608 | bytes 33554688 | tf_op jit(solution)/shard_map/jit(_take)/select_n | solution.py:19
  38.1 8.2 %fusion.36 = (f32[16,2,8,8]{2,3,1,0:T(8,128)S(1)}, f32[16,2,8,8,1032]{4,2,3,1,0:T(8,128)}) fusion(pred[16,8,1032]{2,1,0:T(8,128)(4,1)S(1)} %broadcast_or_fusion, bf16[16,2,2,8,128]{4,3,2,0,1:T(8,128)(2,1)S(1)} %bitcast.89, bf16[16,2,2,1024,128]{4,3,2,0,1:T(8,128)(2,1)} %bitcast.83, bf16[1,1,16,8,16,128]{5,4,3,2,1,0:T(8,128)(2,1)S(1)} %copy-done.3), kind=kOutput, calls=%fused_computation.56 | convolution fusion | flops 566428672 | bytes 26027008 | tf_op jit(solution)/shard_map/sub | solution.py:35
  46.3 7.1 %divide_convert_fusion = bf16[16,2,8,8,1032]{4,2,3,1,0:T(8,128)(2,1)} fusion(f32[16,2,8,8,1032]{4,2,3,1,0:T(8,128)} %get-tuple-element.8, f32[16,2,8,8]{2,3,1,0:T(8,128)S(1)} %get-tuple-element.7), kind=kLoop, calls=%fused_computation.10 | loop fusion | flops 4227072 | bytes 12689408 | tf_op jit(solution)/shard_map/convert_element_type | solution.py:36
  53.5 6.3 %fusion.21 = bf16[16,2,128,8,8]{2,4,3,1,0:T(8,128)(2,1)S(1)} fusion(bf16[16,2,8,8,1032]{4,2,3,1,0:T(8,128)(2,1)} %divide_convert_fusion, bf16[16,2,2,1024,128]{4,3,2,0,1:T(8,128)(2,1)} %bitcast.84, bf16[16,2,2,8,128]{4,3,2,0,1:T(8,128)(2,1)S(1)} %bitcast.90), kind=kOutput, calls=%fused_computation.30 | convolution fusion | flops 558235648 | bytes 21659648 | tf_op jit(solution)/shard_map/rkgwt,rktd->rwkgd/dot_general | solution.py:37
  59.7 1.1 copy.27
  61.0 1.9 gather_fusion.1
  63.1 70.5 %all-gather.2.cloned.1.call-done = bf16[256,8,2048]{2,0,1:T(8,128)(2,1)} async-done(((bf16[16,8,2048]{2,0,1:T(8,128)(2,1)}), bf16[256,8,2048]{2,0,1:T(8,128)(2,1)}) %all-gather.2.cloned.1.call-update) | async-done | bytes 8388624 | tf_op jit(solution)/shard_map/all_gather | solution.py:75
  133.5 8.5 %multiply_reduce_fusion = f32[256,8,64]{0,2,1:T(8,128)S(1)} fusion(bf16[256,8,2048]{2,0,1:T(8,128)(2,1)} %all-gather.2.cloned.1.call-done, bf16[8,64,2048]{2,1,0:T(8,128)(2,1)} %param.20, f32[256,8]{0,1:T(8,128)S(1)} %get-tuple-element.5), kind=kOutput, calls=%fused_computation.27 | convolution fusion | flops 4296933376 | bytes 11018240 | tf_op jit(solution)/shard_map/dot_general | solution.py:85
  142.1 17.1 %all-reduce.1 = bf16[256,8,64]{0,2,1:T(8,128)(2,1)S(1)} all-reduce(f32[256,8,64]{0,2,1:T(8,128)S(1)} %multiply_reduce_fusion), channel_id=1, replica_groups=mesh['section'=2,'tp'=4,'pool'=16] {'tp'}, use_global_device_ids=true, to_apply=%region_4.5 | all-reduce | flops 131072 | bytes 786432 | tf_op jit(solution)/shard_map/psum | solution.py:90
  159.5 2.3 broadcast_multiply_fusion
  161.8 6.5 %mul.56 = bf16[2048,512]{1,0:T(8,128)(2,1)} reshape(bf16[256,8,8,64]{3,2,1,0:T(8,128)(2,1)} %broadcast_multiply_fusion) | data formatting | bytes 4194304 | tf_op jit(solution)/shard_map/mul | solution.py:92
  168.3 8.4 %convolution_convert_fusion = bf16[2048,2048]{1,0:T(8,128)(2,1)} fusion(bf16[2048,512]{1,0:T(8,128)(2,1)} %mul.56, bf16[512,2048]{1,0:T(8,128)(2,1)S(1)} %bitcast.80), kind=kOutput, calls=%fused_computation.22 | convolution fusion | flops 4299161600 | bytes 12582912 | tf_op jit(solution)/shard_map/dot_general | solution.py:96
  176.7 5.3 %all-to-all-start = ((bf16[16,128,2048]{2,1,0:T(8,128)(2,1)}), bf16[16,128,2048]{2,1,0:T(8,128)(2,1)}, u32[]{:S(2)}, u32[]{:S(2)}) async-start(bf16[16,128,2048]{2,1,0:T(8,128)(2,1)} %bitcast.85), calls=%async_computation.1 | async-start | bytes 16777216 | tf_op jit(solution)/shard_map/all_to_all | solution.py:101
  182.0 17.0 %fusion.1 = f32[128,8192]{1,0:T(8,128)} fusion(bf16[128,2048]{1,0:T(8,128)(2,1)S(1)} %bitcast.87, bf16[1,2048,8192]{2,1,0:T(8,128)(2,1)} %param.19), kind=kOutput, calls=%fused_computation.3 | convolution fusion | flops 4294967296 | bytes 38273024 | tf_op jit(solution)/shard_map/dot_general | solution.py:68
  199.1 100.1 %all-to-all-done = bf16[16,128,2048]{2,1,0:T(8,128)(2,1)} async-done(((bf16[16,128,2048]{2,1,0:T(8,128)(2,1)}), bf16[16,128,2048]{2,1,0:T(8,128)(2,1)}, u32[]{:S(2)}, u32[]{:S(2)}) %all-to-all-start) | async-done | bytes 8388640 | tf_op jit(solution)/shard_map/all_to_all | solution.py:101
  299.2 5.3 %convert_reduce_fusion = f32[128,2048]{1,0:T(8,128)S(1)} fusion(bf16[16,128,2048]{2,1,0:T(8,128)(2,1)} %all-to-all-done), kind=kLoop, calls=%fused_computation.8 | loop fusion | flops 8126464 | bytes 9437184 | tf_op jit(solution)/shard_map/reduce_sum | solution.py:104
  304.5 1.5 fusion.27
  306.1 4.9 %collective-permute-start = (bf16[128,2048]{1,0:T(8,128)(2,1)S(1)}, bf16[128,2048]{1,0:T(8,128)(2,1)S(1)}, u32[]{:S(2)}, u32[]{:S(2)}) collective-permute-start(bf16[128,2048]{1,0:T(8,128)(2,1)S(1)} %fusion.27), channel_id=1, source_target_pairs={{0,64},{64,0},{1,65},{65,1},{2,66},{66,2},{3,67},{67,3},{4,68},{68... | collective-permute-start | bytes 1572872 | tf_op jit(solution)/shard_map/ppermute | solution.py:10
  311.0 1.5 collective-permute-done
  312.5 0.8 copy.49
  (27 shorter events, 1.6 us)
Async XLA Ops:
  7.4 160.9 %copy-start = (bf16[8,64,2048]{2,1,0:T(8,128)(2,1)S(1)}, bf16[8,64,2048]{2,1,0:T(8,128)(2,1)}, u32[]{:S(2)}) copy-start(bf16[8,64,2048]{2,1,0:T(8,128)(2,1)} %param.21) | copy-start | bytes 6291460
  7.4 126.2 %all-gather.2.cloned.1.call-start = ((), (), s32[]{:S(2)}) async-start(), calls=%async_computation.3 | async-start | bytes 8912896 | tf_op jit(solution)/shard_map/all_gather | solution.py:75
  23.8 14.3 %copy-start.3 = (bf16[1,1,16,8,16,128]{5,4,3,2,1,0:T(8,128)(2,1)S(1)}, bf16[1,1,16,8,16,128]{5,4,3,2,1,0:T(8,128)(2,1)}, u32[]{:S(2)}) copy-start(bf16[1,1,16,8,16,128]{5,4,3,2,1,0:T(8,128)(2,1)} %param.12) | copy-start | bytes 1572868
  53.5 7.4 %copy-start.2 = (s32[2,16,16]{2,1,0:T(8,128)S(1)}, s32[2,16,16]{2,1,0:T(8,128)}, u32[]{:S(2)}) copy-start(s32[2,16,16]{2,1,0:T(8,128)} %param.17) | copy-start | bytes 6148
  53.5 7.5 %copy-start.1 = (s32[256]{0:T(256)S(1)}, s32[256]{0:T(256)}, u32[]{:S(2)}) copy-start(s32[256]{0:T(256)} %param.18) | copy-start | bytes 3076
  176.7 122.5 %all-to-all-start = ((bf16[16,128,2048]{2,1,0:T(8,128)(2,1)}), bf16[16,128,2048]{2,1,0:T(8,128)(2,1)}, u32[]{:S(2)}, u32[]{:S(2)}) async-start(bf16[16,128,2048]{2,1,0:T(8,128)(2,1)} %bitcast.85), calls=%async_computation.1 | async-start | bytes 16777216 | tf_op jit(solution)/shard_map/all_to_all | solution.py:101
  182.0 122.5 %reduce-scatter.2.cloned.1.call-start = ((), (), s32[]{:S(2)}) async-start(), calls=%async_computation.2 | async-start | bytes 5242880 | tf_op jit(solution)/shard_map/reduce_scatter | solution.py:69
  306.1 6.5 %collective-permute-start = (bf16[128,2048]{1,0:T(8,128)(2,1)S(1)}, bf16[128,2048]{1,0:T(8,128)(2,1)S(1)}, u32[]{:S(2)}, u32[]{:S(2)}) collective-permute-start(bf16[128,2048]{1,0:T(8,128)(2,1)S(1)} %fusion.27), channel_id=1, source_target_pairs={{0,64},{64,0},{1,65},{65,1},{2,66},{66,2},{3,67},{67,3},{4,68},{68... | collective-permute-start | bytes 1572872 | tf_op jit(solution)/shard_map/ppermute | solution.py:10
Sparse Core Ops, SparseCore 0:
  61.0 72.5 all-gather.1
Sparse Core Ops, SparseCore 1:
  199.1 51.5 reduce-scatter.1
where the time goes:
time: 321 us
  waiting for transfers between devices  172 us (54%)
  matrix products  48.3 us (15%)
  other arithmetic  32.9 us (10%)
  local copies, waits for them, and re-layouts  25 us (8%)
  blocking collectives  17.1 us (5%)
  between operations  15 us (5%)
  starting transfers between devices  10.3 us (3%)
    all_to_all x1, waiting for transfers between devices, per_device(): lax.all_to_all(product.astype(jnp.bfloat16), 'pool', split_axis=0, concat...  100 us
    all_gather x1, waiting for transfers between devices, per_device(): everyone = lax.all_gather(context, 'pool', axis=0, tiled=True)  70.5 us
    psum x1, blocking collectives, per_device(): rank_hidden = lax.psum(rank_hidden, 'tp')  17.1 us
    dot_general x1, matrix products, per_device(): partial_out = jnp.dot(flat_rows, wo[0], preferred_element_type=jnp.float32)  17 us
    select_n x2, other arithmetic, attend(): picked = jnp.take(cache_pages, page_rows, axis=0)  15 us
    gather x1, local copies, waits for them, and re-layouts, attend(): picked = jnp.take(cache_pages, page_rows, axis=0)  13.1 us
    dot_general x1, matrix products, per_device(): lax.dot_general(everyone, stacked_down, (((2,), (1,)), ((), ())), preferr...  8.55 us
    dot_general x1, matrix products, per_device(): jnp.dot(broadcast_rows, adapter_up.reshape(pages_per_member * rank_width,...  8.36 us
  transfers between devices with their start and end apart: 4, of which 3 were waited for; matrix products, arithmetic and copies ran while one was open for 8% of the time, Pallas kernels for 0%

commit v1 on v0

--- a/solution.py
+++ b/solution.py
@@ -72,7 +72,10 @@
     output_width = adapter_up.shape[2]
     adapters = layer_page_slot.shape[0] // section_count
     layer_start = section_index * adapters
-    everyone = lax.all_gather(context, "pool", axis=0, tiled=True)
+    n_dev = lax.axis_size("pool")
+    shards = jnp.stack([context for _ in range(n_dev)])
+    shards = lax.all_to_all(shards, "pool", split_axis=0, concat_axis=0)
+    everyone = jnp.concatenate(shards, axis=0)
     total_requests = everyone.shape[0]
     all_slots = layer_page_slot[layer_start + request_adapter[section_index]].reshape(
         total_requests

time: 321 us -> 391 us (1.22)
  waiting for transfers between devices: 172 us -> 222 us
  local copies, waits for them, and re-layouts: 25 us -> 36.9 us
  starting transfers between devices: 10.3 us -> 19.3 us
    all_to_all x0 -> x1, waiting for transfers between devices: none -> 120 us  [per_device(): shards = lax.all_to_all(shards, 'pool', split_axis=0, concat_axis=0)]
    all_gather x1 -> x0, waiting for transfers between devices: 70.5 us -> none  [per_device(): everyone = lax.all_gather(context, 'pool', axis=0, tiled=True)]
    all_to_all x0 -> x1, local copies, waits for them, and re-layouts: none -> 8.4 us  [per_device(): shards = lax.all_to_all(shards, 'pool', split_axis=0, concat_axis=0)]
    all_to_all x0 -> x1, starting transfers between devices: none -> 7.63 us  [per_device(): shards = lax.all_to_all(shards, 'pool', split_axis=0, concat_axis=0)]
    another operation x0 -> x1, local copies, waits for them, and re-layouts: none -> 4.28 us  [per_device(): shards = jnp.stack([context for _ in range(n_dev)])]
  transfers between devices with their start and end apart: 4 -> 4, of which waited for: 3 -> 3; matrix products, arithmetic and copies ran while one was open for 8% -> 6% of each run, Pallas kernels for 0% -> 0%
where the time goes in v1:
time: 391 us; the launch traced here: 390 us
  waiting for transfers between devices  222 us (57%)
  matrix products  48 us (12%)
  local copies, waits for them, and re-layouts  36.9 us (9%)
  other arithmetic  32.9 us (8%)
  starting transfers between devices  19.3 us (5%)
  blocking collectives  17.6 us (5%)
  between operations  13.5 us (3%)
    all_to_all x1, waiting for transfers between devices, per_device(): shards = lax.all_to_all(shards, 'pool', split_axis=0, concat_axis=0)  120 us
    all_to_all x1, waiting for transfers between devices, per_device(): lax.all_to_all(product.astype(jnp.bfloat16), 'pool', split_axis=0, concat...  99.5 us
    psum x1, blocking collectives, per_device(): rank_hidden = lax.psum(rank_hidden, 'tp')  17.6 us
    dot_general x1, matrix products, per_device(): partial_out = jnp.dot(flat_rows, wo[0], preferred_element_type=jnp.float32)  17 us
    select_n x2, other arithmetic, attend(): picked = jnp.take(cache_pages, page_rows, axis=0)  15 us
    gather x1, local copies, waits for them, and re-layouts, attend(): picked = jnp.take(cache_pages, page_rows, axis=0)  13.1 us
    all_to_all x1, local copies, waits for them, and re-layouts, per_device(): shards = lax.all_to_all(shards, 'pool', split_axis=0, concat_axis=0)  8.4 us
    dot_general x1, matrix products, per_device(): jnp.dot(broadcast_rows, adapter_up.reshape(pages_per_member * rank_width,...  8.36 us
  transfers between devices with their start and end apart: 4, of which 3 were waited for; matrix products, arithmetic and copies ran while one was open for 6% of the time, Pallas kernels for 0%

profile of v1, /device:TPU:35, one launch (start us, length us, event | category | flops | bytes accessed | tf_op | source)
XLA Modules:
  0.0 389.7 jit_solution(10763987690690736051)
XLA Ops:
  6.5 0.8 compare_select_fusion.1
  8.2 0.9 copy.46
  9.8 13.1 %gather_fusion = bf16[256,2,2,64,128]{4,3,2,1,0:T(8,128)(2,1)} fusion(bf16[128,2,2,64,128]{4,3,2,1,0:T(8,128)(2,1)} %bitcast.81, s32[1024]{0:T(1024)S(1)} %pad_clamp_fusion.1), kind=kCustom, calls=%fused_computation | custom fusion | bytes 33555456 | tf_op jit(solution)/shard_map/jit(_take)/gather | solution.py:19
  23.0 14.2 %copy_select_fusion = bf16[16,16,2,2,64,128]{5,4,1,3,0,2:T(8,128)(2,1)} fusion(bf16[16,16,2,2,64,128]{5,4,3,2,1,0:T(8,128)(2,1)} %bitcast.80, pred[16,16]{1,0:T(8,128)(4,1)S(1)} %compare_and_fusion), kind=kLoop, calls=%fused_computation.7 | loop fusion | flops 8388608 | bytes 33554688 | tf_op jit(solution)/shard_map/jit(_take)/select_n | solution.py:19
  37.3 8.2 %fusion.32 = (f32[16,2,8,8]{2,3,1,0:T(8,128)S(1)}, f32[16,2,8,8,1032]{4,2,3,1,0:T(8,128)}) fusion(pred[16,8,1032]{2,1,0:T(8,128)(4,1)S(1)} %broadcast_or_fusion, bf16[16,2,2,8,128]{4,3,2,0,1:T(8,128)(2,1)S(1)} %bitcast.89, bf16[16,2,2,1024,128]{4,3,2,0,1:T(8,128)(2,1)} %bitcast.82, bf16[1,1,16,8,16,128]{5,4,3,2,1,0:T(8,128)(2,1)S(1)} %copy-done.4), kind=kOutput, calls=%fused_computation.54 | convolution fusion | flops 566428672 | bytes 26027008 | tf_op jit(solution)/shard_map/sub | solution.py:35
  45.5 7.1 %divide_convert_fusion = bf16[16,2,8,8,1032]{4,2,3,1,0:T(8,128)(2,1)} fusion(f32[16,2,8,8,1032]{4,2,3,1,0:T(8,128)} %get-tuple-element.8, f32[16,2,8,8]{2,3,1,0:T(8,128)S(1)} %get-tuple-element.7), kind=kLoop, calls=%fused_computation.10 | loop fusion | flops 4227072 | bytes 12689408 | tf_op jit(solution)/shard_map/convert_element_type | solution.py:36
  52.6 6.2 %fusion.17 = bf16[16,2,128,8,8]{2,4,3,1,0:T(8,128)(2,1)S(1)} fusion(bf16[16,2,8,8,1032]{4,2,3,1,0:T(8,128)(2,1)} %divide_convert_fusion, bf16[16,2,2,1024,128]{4,3,2,0,1:T(8,128)(2,1)} %bitcast.83, bf16[16,2,2,8,128]{4,3,2,0,1:T(8,128)(2,1)S(1)} %bitcast.90), kind=kOutput, calls=%fused_computation.28 | convolution fusion | flops 558235648 | bytes 21659648 | tf_op jit(solution)/shard_map/rkgwt,rktd->rwkgd/dot_general | solution.py:37
  59.2 4.3 %stack.2 = bf16[16,16,8,2048]{3,1,2,0:T(8,128)(2,1)} broadcast(bf16[16,8,2048]{2,0,1:T(8,128)(2,1)S(1)} %copy.27), dimensions={1,2,3} | broadcast | bytes 8912896 | tf_op jit(solution)/shard_map/stack | solution.py:76
  63.4 7.6 %all-to-all-start = ((bf16[16,16,8,2048]{3,1,2,0:T(8,128)(2,1)}), bf16[16,16,8,2048]{3,1,2,0:T(8,128)(2,1)}, u32[]{:S(2)}, u32[]{:S(2)}) async-start(bf16[16,16,8,2048]{3,1,2,0:T(8,128)(2,1)} %stack.2), calls=%async_computation.1 | async-start | bytes 16777216 | tf_op jit(solution)/shard_map/all_to_all | solution.py:77
  71.2 1.9 gather_fusion.1
  73.3 120.4 %all-to-all-done = bf16[16,16,8,2048]{3,1,2,0:T(8,128)(2,1)} async-done(((bf16[16,16,8,2048]{3,1,2,0:T(8,128)(2,1)}), bf16[16,16,8,2048]{3,1,2,0:T(8,128)(2,1)}, u32[]{:S(2)}, u32[]{:S(2)}) %all-to-all-start) | async-done | bytes 8388640 | tf_op jit(solution)/shard_map/all_to_all | solution.py:77
  193.7 8.4 %copy.28 = bf16[16,16,8,2048]{3,1,0,2:T(8,128)(2,1)} copy(bf16[16,16,8,2048]{3,1,2,0:T(8,128)(2,1)} %all-to-all-done) | data formatting | bytes 16777216 | tf_op jit(solution)/shard_map/all_to_all | solution.py:77
  202.1 8.2 %multiply_reduce_fusion = f32[256,8,64]{0,2,1:T(8,128)S(1)} fusion(bf16[256,8,2048,1]{2,0,3,1:T(8,128)(2,1)} %bitcast.85, bf16[8,64,2048]{2,1,0:T(8,128)(2,1)S(1)} %copy-done.3, f32[256,8]{0,1:T(8,128)S(1)} %get-tuple-element.5), kind=kOutput, calls=%fused_computation.25 | convolution fusion | flops 4296933376 | bytes 11018240 | tf_op jit(solution)/shard_map/dot_general | solution.py:88
  210.3 17.6 %all-reduce.1 = bf16[256,8,64]{0,2,1:T(8,128)(2,1)S(1)} all-reduce(f32[256,8,64]{0,2,1:T(8,128)S(1)} %multiply_reduce_fusion), channel_id=1, replica_groups=mesh['section'=2,'tp'=4,'pool'=16] {'tp'}, use_global_device_ids=true, to_apply=%region_4.5 | all-reduce | flops 131072 | bytes 786432 | tf_op jit(solution)/shard_map/psum | solution.py:93
  228.2 2.3 broadcast_multiply_fusion
  230.5 6.5 %mul.56 = bf16[2048,512]{1,0:T(8,128)(2,1)} reshape(bf16[256,8,8,64]{3,2,1,0:T(8,128)(2,1)} %broadcast_multiply_fusion) | data formatting | bytes 4194304 | tf_op jit(solution)/shard_map/mul | solution.py:95
  237.0 8.4 %convolution_convert_fusion = bf16[2048,2048]{1,0:T(8,128)(2,1)} fusion(bf16[2048,512]{1,0:T(8,128)(2,1)} %mul.56, bf16[512,2048]{1,0:T(8,128)(2,1)S(1)} %bitcast.79), kind=kOutput, calls=%fused_computation.20 | convolution fusion | flops 4299161600 | bytes 12582912 | tf_op jit(solution)/shard_map/dot_general | solution.py:99
  245.4 6.1 %all-to-all-start.1 = ((bf16[16,128,2048]{2,1,0:T(8,128)(2,1)}), bf16[16,128,2048]{2,1,0:T(8,128)(2,1)}, u32[]{:S(2)}, u32[]{:S(2)}) async-start(bf16[16,128,2048]{2,1,0:T(8,128)(2,1)} %bitcast.84), calls=%async_computation.2 | async-start | bytes 16777216 | tf_op jit(solution)/shard_map/all_to_all | solution.py:104
  251.5 17.0 %fusion.1 = f32[128,8192]{1,0:T(8,128)} fusion(bf16[128,2048]{1,0:T(8,128)(2,1)S(1)} %bitcast.87, bf16[1,2048,8192]{2,1,0:T(8,128)(2,1)} %param.19), kind=kOutput, calls=%fused_computation.3 | convolution fusion | flops 4294967296 | bytes 38273024 | tf_op jit(solution)/shard_map/dot_general | solution.py:68
  268.5 99.5 %all-to-all-done.1 = bf16[16,128,2048]{2,1,0:T(8,128)(2,1)} async-done(((bf16[16,128,2048]{2,1,0:T(8,128)(2,1)}), bf16[16,128,2048]{2,1,0:T(8,128)(2,1)}, u32[]{:S(2)}, u32[]{:S(2)}) %all-to-all-start.1) | async-done | bytes 8388640 | tf_op jit(solution)/shard_map/all_to_all | solution.py:104
  368.1 5.3 %convert_reduce_fusion = f32[128,2048]{1,0:T(8,128)S(1)} fusion(bf16[16,128,2048]{2,1,0:T(8,128)(2,1)} %all-to-all-done.1), kind=kLoop, calls=%fused_computation.8 | loop fusion | flops 8126464 | bytes 9437184 | tf_op jit(solution)/shard_map/reduce_sum | solution.py:107
  373.4 1.5 fusion.23
  374.9 5.6 %collective-permute-start = (bf16[128,2048]{1,0:T(8,128)(2,1)S(1)}, bf16[128,2048]{1,0:T(8,128)(2,1)S(1)}, u32[]{:S(2)}, u32[]{:S(2)}) collective-permute-start(bf16[128,2048]{1,0:T(8,128)(2,1)S(1)} %fusion.23), channel_id=1, source_target_pairs={{0,64},{64,0},{1,65},{65,1},{2,66},{66,2},{3,67},{67,3},{4,68},{68... | collective-permute-start | bytes 1572872 | tf_op jit(solution)/shard_map/ppermute | solution.py:10
  380.5 1.5 collective-permute-done
  (30 shorter events, 3.4 us)
Async XLA Ops:
  6.5 230.5 %copy-start = (bf16[8,64,2048]{2,1,0:T(8,128)(2,1)S(1)}, bf16[8,64,2048]{2,1,0:T(8,128)(2,1)}, u32[]{:S(2)}) copy-start(bf16[8,64,2048]{2,1,0:T(8,128)(2,1)} %param.21) | copy-start | bytes 6291460
  23.0 14.3 %copy-start.4 = (bf16[1,1,16,8,16,128]{5,4,3,2,1,0:T(8,128)(2,1)S(1)}, bf16[1,1,16,8,16,128]{5,4,3,2,1,0:T(8,128)(2,1)}, u32[]{:S(2)}) copy-start(bf16[1,1,16,8,16,128]{5,4,3,2,1,0:T(8,128)(2,1)} %param.12) | copy-start | bytes 1572868
  63.4 7.6 %copy-start.2 = (s32[2,16,16]{2,1,0:T(8,128)S(1)}, s32[2,16,16]{2,1,0:T(8,128)}, u32[]{:S(2)}) copy-start(s32[2,16,16]{2,1,0:T(8,128)} %param.17) | copy-start | bytes 6148
  63.4 7.8 %copy-start.1 = (s32[256]{0:T(256)S(1)}, s32[256]{0:T(256)}, u32[]{:S(2)}) copy-start(s32[256]{0:T(256)} %param.18) | copy-start | bytes 3076
  63.4 130.3 %all-to-all-start = ((bf16[16,16,8,2048]{3,1,2,0:T(8,128)(2,1)}), bf16[16,16,8,2048]{3,1,2,0:T(8,128)(2,1)}, u32[]{:S(2)}, u32[]{:S(2)}) async-start(bf16[16,16,8,2048]{3,1,2,0:T(8,128)(2,1)} %stack.2), calls=%async_computation.1 | async-start | bytes 16777216 | tf_op jit(solution)/shard_map/all_to_all | solution.py:77
  193.7 8.4 %copy-start.3 = (bf16[8,64,2048]{2,1,0:T(8,128)(2,1)S(1)}, bf16[8,64,2048]{2,1,0:T(8,128)(2,1)}, u32[]{:S(2)}) copy-start(bf16[8,64,2048]{2,1,0:T(8,128)(2,1)} %param.20) | copy-start | bytes 6291460
  245.4 122.7 %all-to-all-start.1 = ((bf16[16,128,2048]{2,1,0:T(8,128)(2,1)}), bf16[16,128,2048]{2,1,0:T(8,128)(2,1)}, u32[]{:S(2)}, u32[]{:S(2)}) async-start(bf16[16,128,2048]{2,1,0:T(8,128)(2,1)} %bitcast.84), calls=%async_computation.2 | async-start | bytes 16777216 | tf_op jit(solution)/shard_map/all_to_all | solution.py:104
  251.4 121.9 %reduce-scatter.2.cloned.1.call-start = ((), (), s32[]{:S(2)}) async-start(), calls=%async_computation.3 | async-start | bytes 5242880 | tf_op jit(solution)/shard_map/reduce_scatter | solution.py:69
  374.9 7.1 %collective-permute-start = (bf16[128,2048]{1,0:T(8,128)(2,1)S(1)}, bf16[128,2048]{1,0:T(8,128)(2,1)S(1)}, u32[]{:S(2)}, u32[]{:S(2)}) collective-permute-start(bf16[128,2048]{1,0:T(8,128)(2,1)S(1)} %fusion.23), channel_id=1, source_target_pairs={{0,64},{64,0},{1,65},{65,1},{2,66},{66,2},{3,67},{67,3},{4,68},{68... | collective-permute-start | bytes 1572872 | tf_op jit(solution)/shard_map/ppermute | solution.py:10
Sparse Core Ops, SparseCore 0:
  268.6 51.9 reduce-scatter.1
